TPU v7x, 32 devices: a whole 2x2x4 slice. The times are simulated.
32 devices in a mesh: pq: 2 (over x), rs: 16 (over z, y, core).
Axes of the slice: x: 2, y: 2, z: 4, core: 2. Of those that a mesh axis runs over, the one named last changes fastest.
Arguments:
- integrals: bfloat16 [128, 1152, 1152], P('pq', 'rs'), may hold values from -6 to 6
- coeff: bfloat16 [1152, 896], P('rs', 'pq'), may hold values from -0.1875 to 0.1875
Outputs:
- half_mo: bfloat16 [128, 896, 896], P('pq', 'rs')
All inputs are finite; a program needn't handle non-finite values.
Results may differ from a plain program's by a relative error of at most 0.0049.
Values may be sent and summed in bfloat16 or wider, within the bound.
A program may use at most 128 MiB of HBM per device.

v0:
```python
import jax
import jax.numpy as jnp
from jax import lax
from jax.sharding import PartitionSpec as P

NBASIS = 1152
NORB = 896


def second_half(received, panel):
    return jnp.einsum("prl,rk->plk", received, panel, preferred_element_type=jnp.float32).astype(
        jnp.bfloat16
    )


def on_device(integrals, coeff):
    pair_rows = integrals.shape[0]
    block_rows = integrals.shape[1]
    flat = integrals.reshape(pair_rows * block_rows, NBASIS)
    strip = lax.all_gather(coeff, "pq", axis=1, tiled=True)
    panel = lax.all_gather(strip, "rs", axis=0, tiled=True)
    first = jnp.dot(flat, panel, preferred_element_type=jnp.float32).astype(jnp.bfloat16)
    first = first.reshape(pair_rows, block_rows, NORB)
    return second_half(lax.all_to_all(first, "rs", split_axis=2, concat_axis=1, tiled=True), panel)


def solution(mesh):
    placed = (P("pq", "rs", None), P("rs", "pq"))
    return jax.shard_map(
        on_device, mesh=mesh, in_specs=placed, out_specs=P("pq", "rs", None), check_vma=False
    )
```

profile of v0, /device:TPU:1, one launch (start us, length us, event | category | flops | bytes accessed | tf_op | source)
XLA Modules:
  0.0 468.6 jit_solution(1243256376461925950)
XLA Ops:
  6.5 0.0 all-gather.3.cloned.1.call-start
  6.5 4.7 %all-gather = bf16[2,448,72]{1,2,0:T(8,128)(2,1)S(1)} all-gather(bf16[1,448,72]{1,2,0:T(8,128)(2,1)} %bitcast.25), channel_id=1, replica_groups=mesh['pq'=2,'rs'=16] {'pq'}, dimensions={0}, use_global_device_ids=true | all-gather | bytes 193536 | tf_op jit(solution)/shard_map/all_gather | solution.py:20
  11.2 0.1 copy.7
  11.3 0.8 reshape.9
  12.1 0.0 all-gather.3.cloned.1.call-update
  12.2 44.5 %all-gather.3.cloned.1.call-done = bf16[1152,896]{1,0:T(8,128)(2,1)} async-done(((bf16[72,896]{1,0:T(8,128)(2,1)}), bf16[1152,896]{1,0:T(8,128)(2,1)}) %all-gather.3.cloned.1.call-update) | async-done | bytes 2064400 | tf_op jit(solution)/shard_map/all_gather | solution.py:21
  56.7 17.5 %convolution_convert_fusion = bf16[4608,896]{1,0:T(8,128)(2,1)} fusion(bf16[4608,1152]{1,0:T(8,128)(2,1)} %bitcast.26, bf16[1152,896]{1,0:T(8,128)(2,1)} %all-gather.3.cloned.1.call-done), kind=kOutput, calls=%fused_computation | convolution fusion | flops 9516810240 | bytes 20938752 | tf_op jit(solution)/shard_map/dot_general | solution.py:22
  74.2 18.5 %copy.8 = bf16[64,72,896]{1,0,2:T(8,128)(2,1)} copy(bf16[64,72,896]{2,1,0:T(8,128)(2,1)} %bitcast.23) | data formatting | bytes 16515072 | tf_op jit(solution)/shard_map/reshape | solution.py:23
  92.7 321.5 %all_to_all.18 = bf16[64,72,896]{1,0,2:T(8,128)(2,1)S(1)} all-to-all(bf16[64,72,896]{1,0,2:T(8,128)(2,1)} %copy.8), channel_id=1, replica_groups=mesh['pq'=2,'rs'=16] {'rs'}, dimensions={2} | all-to-all | bytes 16515072 | tf_op jit(solution)/shard_map/all_to_all | solution.py:24
  414.1 10.6 %copy.10 = bf16[64,16,72,56]{2,1,3,0:T(8,128)(2,1)} copy(bf16[64,16,72,56]{2,0,3,1:T(8,128)(2,1)S(1)} %bitcast.22) | data formatting | bytes 16515072 | tf_op jit(solution)/shard_map/all_to_all | solution.py:24
  424.7 0.0 copy-start
  424.7 23.2 %all_to_all.16 = bf16[64,1152,56]{1,2,0:T(8,128)(2,1)} reshape(bf16[64,16,72,56]{2,1,3,0:T(8,128)(2,1)} %copy.10) | data formatting | bytes 16515072 | tf_op jit(solution)/shard_map/all_to_all | solution.py:24
  447.9 0.0 copy-done
  447.9 13.8 %convolution_convert_fusion.1 = bf16[64,56,896]{2,1,0:T(8,128)(2,1)} fusion(bf16[64,1152,56]{1,2,0:T(8,128)(2,1)} %all_to_all.16, bf16[1152,896]{1,0:T(8,128)(2,1)S(1)} %copy-done), kind=kOutput, calls=%fused_computation.1 | convolution fusion | flops 7401963520 | bytes 16744448 | tf_op jit(solution)/shard_map/prl,rk->plk/dot_general | solution.py:11
Async XLA Ops:
  6.5 50.2 %all-gather.3.cloned.1.call-start = ((), (), s32[]{:S(2)}) async-start(), calls=%async_computation.1 | async-start | bytes 2193408 | tf_op jit(solution)/shard_map/all_gather | solution.py:21
  424.7 23.2 %copy-start = (bf16[1152,896]{1,0:T(8,128)(2,1)S(1)}, bf16[1152,896]{1,0:T(8,128)(2,1)}, u32[]{:S(2)}) copy-start(bf16[1152,896]{1,0:T(8,128)(2,1)} %all-gather.3.cloned.1.call-done) | copy-start | bytes 6193156
Sparse Core Ops, SparseCore 0:
  12.3 44.3 all-gather.2
where the time goes:
time: 470 us; the launch traced here: 469 us
  blocking collectives  326 us (69%)
  local copies, waits for them, and re-layouts  53.2 us (11%)
  waiting for transfers between devices  44.6 us (9%)
  matrix products  31.3 us (7%)
  between operations  13.4 us (3%)
    all_to_all x1, blocking collectives, on_device(): lax.all_to_all(first, 'rs', split_axis=2, concat_axis=1, tiled=True)  321 us
    all_gather x1, waiting for transfers between devices, on_device(): panel = lax.all_gather(strip, 'rs', axis=0, tiled=True)  44.5 us
    all_to_all x2, local copies, waits for them, and re-layouts, on_device(): lax.all_to_all(first, 'rs', split_axis=2, concat_axis=1, tiled=True)  33.8 us
    reshape x1, local copies, waits for them, and re-layouts, on_device(): first = first.reshape(pair_rows, block_rows, NORB)  18.5 us
    dot_general x1, matrix products, on_device(): jnp.dot(flat, panel, preferred_element_type=jnp.float32)  17.5 us
    dot_general x1, matrix products, second_half(): jnp.einsum('prl,rk->plk', received, panel, preferred_element_type=jnp.flo...  13.8 us
  transfers between devices with their start and end apart: 1, of which 1 were waited for; matrix products, arithmetic and copies ran while one was open for 0% of the time, Pallas kernels for 0%

commit v1 on v0

--- a/solution.py
+++ b/solution.py
@@ -21,7 +21,13 @@
     panel = lax.all_gather(strip, "rs", axis=0, tiled=True)
     first = jnp.dot(flat, panel, preferred_element_type=jnp.float32).astype(jnp.bfloat16)
     first = first.reshape(pair_rows, block_rows, NORB)
-    return second_half(lax.all_to_all(first, "rs", split_axis=2, concat_axis=1, tiled=True), panel)
+    return second_half(
+        jnp.concatenate(
+            lax.all_to_all(jnp.stack(jnp.split(first, lax.axis_size("rs"), axis=2)), "rs", 0, 0),
+            axis=1,
+        ),
+        panel,
+    )
 
 
 def solution(mesh):

time: 470 us -> 511 us (1.087)
  local copies, waits for them, and re-layouts: 53.2 us -> 97.4 us
    unnamed x3 -> x52, local copies, waits for them, and re-layouts: 0.8 us -> 46.2 us
    all_to_all x2 -> x0, local copies, waits for them, and re-layouts: 33.8 us -> none  [on_device(): lax.all_to_all(first, 'rs', split_axis=2, concat_axis=1, tiled=True)]
    reshape x1 -> x2, local copies, waits for them, and re-layouts: 18.5 us -> 42.7 us  [on_device(): jnp.concatenate(lax.all_to_all(jnp.stack(jnp.split(first, lax.axis_size('...]
    split x0 -> x1, local copies, waits for them, and re-layouts: none -> 8.3 us  [on_device(): jnp.split(first, lax.axis_size('rs'), axis=2)]
where the time goes in v1:
time: 511 us; the launch traced here: 510 us
  blocking collectives  325 us (64%)
  local copies, waits for them, and re-layouts  97.4 us (19%)
  waiting for transfers between devices  44.6 us (9%)
  matrix products  28.9 us (6%)
  between operations  13.6 us (3%)
    all_to_all x1, blocking collectives, on_device(): lax.all_to_all(jnp.stack(jnp.split(first, lax.axis_size('rs'), axis=2)),...  321 us
    unnamed x52, local copies, waits for them, and re-layouts  46.2 us
    all_gather x1, waiting for transfers between devices, on_device(): panel = lax.all_gather(strip, 'rs', axis=0, tiled=True)  44.5 us
    reshape x2, local copies, waits for them, and re-layouts, on_device(): jnp.concatenate(lax.all_to_all(jnp.stack(jnp.split(first, lax.axis_size('...  42.7 us
    dot_general x1, matrix products, on_device(): jnp.dot(flat, panel, preferred_element_type=jnp.float32)  15.1 us
    dot_general x1, matrix products, second_half(): jnp.einsum('prl,rk->plk', received, panel, preferred_element_type=jnp.flo...  13.8 us
  transfers between devices with their start and end apart: 1, of which 1 were waited for; matrix products, arithmetic and copies ran while one was open for 0% of the time, Pallas kernels for 0%

profile of v1, /device:TPU:1, one launch (start us, length us, event | category | flops | bytes accessed | tf_op | source)
XLA Modules:
  0.0 510.0 jit_solution(11067591270855484033)
XLA Ops:
  6.5 0.0 all-gather.3.cloned.1.call-start
  6.5 4.7 all-gather
  11.2 0.1 copy.5
  11.3 0.8 reshape.17
  12.1 0.0 all-gather.3.cloned.1.call-update
  12.2 44.5 %all-gather.3.cloned.1.call-done = bf16[1152,896]{1,0:T(8,128)(2,1)} async-done(((bf16[72,896]{1,0:T(8,128)(2,1)}), bf16[1152,896]{1,0:T(8,128)(2,1)}) %all-gather.3.cloned.1.call-update) | async-done | bytes 2064400 | tf_op jit(solution)/shard_map/all_gather | solution.py:21
  56.7 15.1 %convolution_convert_fusion = bf16[4608,896]{1,0:T(8,128)(2,1)S(1)} fusion(bf16[4608,1152]{1,0:T(8,128)(2,1)} %bitcast.55, bf16[1152,896]{1,0:T(8,128)(2,1)} %all-gather.3.cloned.1.call-done), kind=kOutput, calls=%fused_computation | convolution fusion | flops 9516810240 | bytes 20938752 | tf_op jit(solution)/shard_map/dot_general | solution.py:22
  71.8 8.3 %fusion.1 = (bf16[64,72,56]{2,1,0:T(8,128)(2,1)}, bf16[64,72,56]{2,1,0:T(8,128)(2,1)}, bf16[64,72,56]{2,1,0:T(8,128)(2,1)}, bf16[64,72,56]{2,1,0:T(8,128)(2,1)},...) fusion(bf16[64,72,896]{2,1,0:T(8,128)(2,1)S(1)} %bitcast.52), kind=kLoop, calls=%fused_computation.19 | loop fusion | bytes 16515072 | tf_op jit(solution)/shard_map/split | solution.py:26
  80.1 2.3 copy.38
  82.5 2.3 copy.37
  84.8 2.3 copy.36
  87.0 2.3 copy.35
  89.3 2.3 copy.34
  91.6 2.3 copy.33
  93.9 2.3 copy.32
  96.2 2.3 copy.31
  98.5 2.3 copy.30
  100.8 2.3 copy.29
  103.1 2.3 copy.28
  105.4 2.3 copy.27
  107.7 2.3 copy.26
  110.0 2.3 copy.25
  112.2 1.3 copy.24
  113.6 0.0 copy-start.3
  113.6 0.0 copy-start.2
  113.6 1.3 copy.23
  114.9 0.0 copy-start.8
  114.9 0.0 copy-start.7
  114.9 0.0 copy-start.6
  114.9 0.0 copy-start.5
  114.9 0.0 copy-start.4
  114.9 0.0 copy-start.1
  114.9 1.4 bitcast_dynamic-update-slice_fusion.15
  116.3 0.0 copy-start
  116.3 1.6 bitcast_dynamic-update-slice_fusion.14
  117.9 1.3 bitcast_dynamic-update-slice_fusion.13
  119.2 1.3 bitcast_dynamic-update-slice_fusion.12
  120.6 1.3 bitcast_dynamic-update-slice_fusion.11
  121.9 1.3 bitcast_dynamic-update-slice_fusion.10
  123.2 1.3 bitcast_dynamic-update-slice_fusion.9
  124.5 0.0 copy-done.8
  124.5 0.1 bitcast_dynamic-update-slice_fusion.8
  124.7 0.0 copy-done.7
  124.7 0.1 bitcast_dynamic-update-slice_fusion.7
  124.8 0.0 copy-done.6
  124.8 0.1 bitcast_dynamic-update-slice_fusion.6
  125.0 0.0 copy-done.5
  125.0 0.1 bitcast_dynamic-update-slice_fusion.5
  125.1 0.0 copy-done.4
  125.1 0.1 bitcast_dynamic-update-slice_fusion.4
  125.3 0.0 copy-done.3
  125.3 0.1 bitcast_dynamic-update-slice_fusion.3
  125.4 0.0 copy-done.2
  125.4 0.1 bitcast_dynamic-update-slice_fusion.2
  125.6 0.0 copy-done.1
  125.6 0.1 bitcast_dynamic-update-slice_fusion.1
  125.7 0.0 copy-done
  125.7 0.1 bitcast_dynamic-update-slice_fusion
  125.9 320.8 %all_to_all.5 = bf16[16,64,72,56]{2,3,1,0:T(8,128)(2,1)S(1)} all-to-all(bf16[16,64,72,56]{2,3,1,0:T(8,128)(2,1)S(1)} %bitcast_dynamic-update-slice_fusion), channel_id=1, replica_groups=mesh['pq'=2,'rs'=16] {'rs'}, dimensions={0} | all-to-all | bytes 16515072 | tf_op jit(solution)/shard_map/all_to_all | solution.py:26
  446.7 19.5 %copy.22 = bf16[64,16,72,56]{2,1,3,0:T(8,128)(2,1)} copy(bf16[64,16,72,56]{2,3,0,1:T(8,128)(2,1)S(1)} %bitcast.51) | data formatting | bytes 16515072 | tf_op jit(solution)/shard_map/reshape | solution.py:25
  466.2 0.0 copy-start.9
  466.2 23.2 %reshape.15 = bf16[64,1152,56]{1,2,0:T(8,128)(2,1)} reshape(bf16[64,16,72,56]{2,1,3,0:T(8,128)(2,1)} %copy.22) | data formatting | bytes 16515072 | tf_op jit(solution)/shard_map/reshape | solution.py:25
  489.4 0.0 copy-done.9
  489.4 13.8 %convolution_convert_fusion.1 = bf16[64,56,896]{2,1,0:T(8,128)(2,1)} fusion(bf16[64,1152,56]{1,2,0:T(8,128)(2,1)} %reshape.15, bf16[1152,896]{1,0:T(8,128)(2,1)S(1)} %copy-done.9), kind=kOutput, calls=%fused_computation.1 | convolution fusion | flops 7401963520 | bytes 16744448 | tf_op jit(solution)/shard_map/prl,rk->plk/dot_general | solution.py:11
Async XLA Ops:
  6.5 50.2 %all-gather.3.cloned.1.call-start = ((), (), s32[]{:S(2)}) async-start(), calls=%async_computation.1 | async-start | bytes 2193408 | tf_op jit(solution)/shard_map/all_gather | solution.py:21
  113.6 11.7 %copy-start.3 = (bf16[64,72,56]{1,2,0:T(8,128)(2,1)S(1)}, bf16[64,72,56]{1,2,0:T(8,128)(2,1)}, u32[]{:S(2)}) copy-start(bf16[64,72,56]{1,2,0:T(8,128)(2,1)} %copy.35) | copy-start | bytes 1548292
  113.6 11.9 %copy-start.2 = (bf16[64,72,56]{1,2,0:T(8,128)(2,1)S(1)}, bf16[64,72,56]{1,2,0:T(8,128)(2,1)}, u32[]{:S(2)}) copy-start(bf16[64,72,56]{1,2,0:T(8,128)(2,1)} %copy.36) | copy-start | bytes 1548292
  114.9 9.6 %copy-start.8 = (bf16[64,72,56]{1,2,0:T(8,128)(2,1)S(1)}, bf16[64,72,56]{1,2,0:T(8,128)(2,1)}, u32[]{:S(2)}) copy-start(bf16[64,72,56]{1,2,0:T(8,128)(2,1)} %copy.30) | copy-start | bytes 1548292
  114.9 9.8 %copy-start.7 = (bf16[64,72,56]{1,2,0:T(8,128)(2,1)S(1)}, bf16[64,72,56]{1,2,0:T(8,128)(2,1)}, u32[]{:S(2)}) copy-start(bf16[64,72,56]{1,2,0:T(8,128)(2,1)} %copy.31) | copy-start | bytes 1548292
  114.9 9.9 %copy-start.6 = (bf16[64,72,56]{1,2,0:T(8,128)(2,1)S(1)}, bf16[64,72,56]{1,2,0:T(8,128)(2,1)}, u32[]{:S(2)}) copy-start(bf16[64,72,56]{1,2,0:T(8,128)(2,1)} %copy.32) | copy-start | bytes 1548292
  114.9 10.1 %copy-start.5 = (bf16[64,72,56]{1,2,0:T(8,128)(2,1)S(1)}, bf16[64,72,56]{1,2,0:T(8,128)(2,1)}, u32[]{:S(2)}) copy-start(bf16[64,72,56]{1,2,0:T(8,128)(2,1)} %copy.33) | copy-start | bytes 1548292
  114.9 10.2 %copy-start.4 = (bf16[64,72,56]{1,2,0:T(8,128)(2,1)S(1)}, bf16[64,72,56]{1,2,0:T(8,128)(2,1)}, u32[]{:S(2)}) copy-start(bf16[64,72,56]{1,2,0:T(8,128)(2,1)} %copy.34) | copy-start | bytes 1548292
  114.9 10.7 %copy-start.1 = (bf16[64,72,56]{1,2,0:T(8,128)(2,1)S(1)}, bf16[64,72,56]{1,2,0:T(8,128)(2,1)}, u32[]{:S(2)}) copy-start(bf16[64,72,56]{1,2,0:T(8,128)(2,1)} %copy.37) | copy-start | bytes 1548292
  116.3 9.4 %copy-start = (bf16[64,72,56]{1,2,0:T(8,128)(2,1)S(1)}, bf16[64,72,56]{1,2,0:T(8,128)(2,1)}, u32[]{:S(2)}) copy-start(bf16[64,72,56]{1,2,0:T(8,128)(2,1)} %copy.38) | copy-start | bytes 1548292
  466.2 23.2 %copy-start.9 = (bf16[1152,896]{1,0:T(8,128)(2,1)S(1)}, bf16[1152,896]{1,0:T(8,128)(2,1)}, u32[]{:S(2)}) copy-start(bf16[1152,896]{1,0:T(8,128)(2,1)} %all-gather.3.cloned.1.call-done) | copy-start | bytes 6193156
Sparse Core Ops, SparseCore 0:
  12.3 44.3 all-gather.2
